TPU v7x, 32 devices: a whole 2x2x4 slice. The times are simulated.
32 devices in a mesh: dp: 4 (over y, x), expert: 8 (over z, core).
Axes of the slice: x: 2, y: 2, z: 4, core: 2. Of those that a mesh axis runs over, the one named last changes fastest.
Arguments:
- hidden: bfloat16 [8, 4608, 1408], P('expert', 'dp')
- upstream: bfloat16 [8, 4608, 2048], P('expert', 'dp')
- token_counts: int32 [8, 4], P('expert', 'dp'), may hold values from 1 to 1152, as said below
- master: float32 [8, 1408, 2048], P('expert', 'dp'), may hold values from -0.15625 to 0.15625
- first_moment: float32 [8, 1408, 2048], P('expert', 'dp'), may hold values from -6 to 6
- second_moment: float32 [8, 1408, 2048], P('expert', 'dp'), may hold values from 0.25 to 4
- router_input: bfloat16 [4096, 2048], P(('dp', 'expert')), may hold values from -6 to 6
- router_cot: bfloat16 [64, 4096], P(None, ('dp', 'expert'))
- router_master: float32 [64, 2048], replicated, may hold values from -0.125 to 0.125
- router_first: float32 [64, 2048], replicated, may hold values from -6 to 6
- router_second: float32 [64, 2048], replicated, may hold values from 0.25 to 4
- partner: int32 [8], replicated, may hold values from 0 to 7, as said below
Outputs:
- new_weight: bfloat16 [8, 1408, 2048], P('expert')
- new_master: float32 [8, 1408, 2048], P('expert', 'dp')
- new_first: float32 [8, 1408, 2048], P('expert', 'dp')
- new_second: float32 [8, 1408, 2048], P('expert', 'dp')
- router_master_new: float32 [64, 2048], replicated
- router_first_new: float32 [64, 2048], replicated
- router_second_new: float32 [64, 2048], replicated
Inputs may be any that keep to these rules, and one draw needn't show every extreme that they name: partner[partner[p]] = p for every position p; a position with partner[p] = p keeps its expert. The first token_counts[e, d] of replica d's 1152 slots for position e are live, the rest are padding.
All inputs are finite; a program needn't handle non-finite values.
Results may differ from a plain program's by a relative error of at most 0.001.
Values may be sent and summed in bfloat16 or wider, within the bound.
A program may use at most 128 MiB of HBM per device.

v0:
```python
import math
import jax
import jax.numpy as jnp
from jax import lax
from jax.sharding import PartitionSpec as P

beta_first = 0.9
beta_second = 0.95
learn_rate = 0.001
decay_weight = 0.1
adam_eps = 1e-08
norm_eps = 1e-06
correct_first = 1.0 - 0.9**10
correct_second = 1.0 - 0.95**10


def adam_update(gradient, moment_one, moment_two, weights):
    first_new = beta_first * moment_one + (1.0 - beta_first) * gradient
    second_new = beta_second * moment_two + (1.0 - beta_second) * gradient * gradient
    ratio = first_new / correct_first / (jnp.sqrt(second_new / correct_second) + adam_eps)
    weights_new = weights - learn_rate * (ratio + decay_weight * weights)
    return (weights_new, first_new, second_new)


code_top = 32767.0
steps_per_octave = 256.0


def scale_of(level):
    return jnp.exp2(level.astype(jnp.float32) * (1.0 / steps_per_octave))


def encode(blocks):
    groups, rows, width = blocks.shape
    peak = jnp.maximum(jnp.max(jnp.abs(blocks), axis=2), 1e-37)
    level = jnp.clip(jnp.ceil(jnp.log2(peak) * steps_per_octave), -32000.0, 32767.0).astype(
        jnp.int16
    )
    scaled = blocks * (code_top / scale_of(level))[:, :, None]
    codes = jnp.clip(jnp.round(scaled), -code_top, code_top).astype(jnp.int16)
    extra = -(-rows // width)
    levels = jnp.pad(level, ((0, 0), (0, extra * width - rows))).reshape(groups, extra, width)
    return jnp.concatenate([codes, levels], axis=1)


def decode(payload, rows):
    groups, _, width = payload.shape
    level = payload[:, rows:].reshape(groups, -1)[:, :rows]
    return payload[:, :rows].astype(jnp.float32) * (scale_of(level) * (1.0 / code_top))[:, :, None]


def to_pieces(matrix, groups):
    rows, width = matrix.shape
    return matrix.reshape(rows, groups, width // groups).swapaxes(0, 1)


def from_pieces(pieces):
    groups, rows, width = pieces.shape
    return pieces.swapaxes(0, 1).reshape(rows, groups * width)


def exchange(payload, axis="expert"):
    return lax.all_to_all(payload, axis, split_axis=0, concat_axis=0, tiled=True)


def regather(weight_shard):
    return lax.all_gather(weight_shard, "dp", axis=0, tiled=True)


def on_device(
    hidden,
    upstream,
    token_counts,
    master,
    first_moment,
    second_moment,
    router_input,
    router_cot,
    router_master,
    router_first,
    router_second,
    partner,
):
    hidden_units = hidden.shape[2]
    features = upstream.shape[2]
    row_count = hidden.shape[1]
    groups = lax.axis_size("expert")
    rows = master.shape[1]
    early_master = exchange(encode(to_pieces(master[0], groups)))
    early_first = exchange(encode(to_pieces(first_moment[0], groups)))
    early_second = exchange(encode(to_pieces(second_moment[0], groups)))
    live_rows = jnp.arange(row_count, dtype=jnp.int32) < token_counts[0, 0]
    activations = hidden[0]
    grads_out = upstream[0]
    masked_out = jnp.where(live_rows[:, None], grads_out, jnp.zeros_like(grads_out))
    router_partial = jnp.dot(router_cot, router_input, preferred_element_type=jnp.float32)
    partial = lax.dot_general(
        activations, masked_out, (((0,), (0,)), ((), ())), preferred_element_type=jnp.float32
    )
    gradient = lax.psum_scatter(partial, "dp", scatter_dimension=0, tiled=True)
    moved_gradient = exchange(encode(to_pieces(gradient, groups)))
    router_grad = lax.psum(router_partial, ("dp", "expert"))
    expert_square = lax.psum(jnp.sum(gradient * gradient), ("dp", "expert"))
    total_square = expert_square + jnp.sum(router_grad * router_grad)
    clip_limit = 2.0 * math.sqrt(
        float(groups * hidden_units * features + router_cot.shape[0] * features)
    )
    factor = jnp.minimum(1.0, clip_limit / (jnp.sqrt(total_square) + norm_eps))
    states = adam_update(
        factor * decode(moved_gradient, rows),
        decode(early_first, rows),
        decode(early_second, rows),
        decode(early_master, rows),
    )
    router_outs = adam_update(factor * router_grad, router_first, router_second, router_master)
    sent = [
        encode(jnp.take(member, partner, axis=0)) for member in (states[0], states[1], states[2])
    ]
    moved = [from_pieces(decode(exchange(payload), rows)) for payload in sent]
    moved_weight = regather(moved[0].astype(jnp.bfloat16))
    return (
        moved_weight[None],
        moved[0][None],
        moved[1][None],
        moved[2][None],
        router_outs[0],
        router_outs[1],
        router_outs[2],
    )


def solution(mesh):
    in_specs = (
        P("expert", "dp", None),
        P("expert", "dp", None),
        P("expert", "dp"),
        P("expert", "dp", None),
        P("expert", "dp", None),
        P("expert", "dp", None),
        P(("dp", "expert"), None),
        P(None, ("dp", "expert")),
        P(),
        P(),
        P(),
        P(),
    )
    out_specs = (
        P("expert", None, None),
        P("expert", "dp", None),
        P("expert", "dp", None),
        P("expert", "dp", None),
        P(),
        P(),
        P(),
    )
    return jax.shard_map(
        on_device, mesh=mesh, in_specs=in_specs, out_specs=out_specs, check_vma=False
    )
```

profile of v0, /device:TPU:0, one launch (start us, length us, event | category | flops | bytes accessed | tf_op | source)
XLA Modules:
  0.0 543.5 jit_solution(693130620030949028)
XLA Ops:
  9.9 12.9 %convolution_bitcast_fusion = f32[1408,2048]{0,1:T(8,128)} fusion(bf16[1,1152,2048]{2,1,0:T(8,128)(2,1)} %param.15, pred[1152]{0:T(1024)(128)(4,1)S(1)} %iota_compare_fusion, bf16[1,1152,1408]{2,1,0:T(8,128)(2,1)S(1)} %copy-done), kind=kOutput, calls=%fused_computation.3 | convolution fusion | flops 6646136832 | bytes 19498112 | tf_op jit(solution)/shard_map/dot_general | solution.py:97
  22.8 12.0 %copy.42 = f32[1408,2048]{1,0:T(8,128)} copy(f32[1408,2048]{0,1:T(8,128)} %convolution_bitcast_fusion) | data formatting | bytes 23068672
  34.9 3.1 copy.50
  40.1 1.2 pad_add_fusion.3
  41.4 6.4 %all-to-all-start.3 = ((s16[8,354,256]{2,1,0:T(8,128)(2,1)}), s16[8,354,256]{2,1,0:T(8,128)(2,1)}, u32[]{:S(2)}, u32[]{:S(2)}) async-start(s16[8,354,256]{2,1,0:T(8,128)(2,1)} %pad_add_fusion.3), calls=%async_computation.3 | async-start | bytes 2949120 | tf_op jit(solution)/shard_map/all_to_all | solution.py:63
  47.7 3.1 copy.47
  54.2 29.3 %all-to-all-done.3 = s16[8,354,256]{2,1,0:T(8,128)(2,1)} async-done(((s16[8,354,256]{2,1,0:T(8,128)(2,1)}), s16[8,354,256]{2,1,0:T(8,128)(2,1)}, u32[]{:S(2)}, u32[]{:S(2)}) %all-to-all-start.3) | async-done | bytes 1450016 | tf_op jit(solution)/shard_map/all_to_all | solution.py:63
  83.5 4.3 all-to-all-start.1
  87.8 3.1 copy.45
  93.1 1.2 pad_add_fusion
  94.3 29.2 %all-to-all-done.1 = s16[8,354,256]{2,1,0:T(8,128)(2,1)} async-done(((s16[8,354,256]{2,1,0:T(8,128)(2,1)}), s16[8,354,256]{2,1,0:T(8,128)(2,1)}, u32[]{:S(2)}, u32[]{:S(2)}) %all-to-all-start.1) | async-done | bytes 1450016 | tf_op jit(solution)/shard_map/all_to_all | solution.py:63
  123.5 4.3 all-to-all-start
  127.8 22.0 %reduce-scatter.4.cloned.1.call-done = f32[352,2048]{1,0:T(8,128)} async-done(((f32[1408,2048]{1,0:T(8,128)}), f32[352,2048]{1,0:T(8,128)}) %reduce-scatter.4.cloned.1.call-update) | async-done | bytes 2883600
  149.8 2.3 copy.43
  152.1 2.3 copy.36
  154.4 2.3 fusion.9
  156.7 2.3 fusion.12
  160.2 3.3 all-to-all-done
  163.5 4.3 all-to-all-start.2
  167.8 2.1 fusion.26
  170.0 141.4 %all-reduce.9.cloned.1.call-done = f32[64,2048]{1,0:T(8,128)} async-done(((f32[64,2048]{1,0:T(8,128)}), f32[64,2048]{1,0:T(8,128)}) %all-reduce.9.cloned.1.call-update) | async-done | bytes 524304 | tf_op jit(solution)/shard_map/psum | solution.py:102
  311.4 1.8 multiply_reduce_fusion.1
  315.6 1.4 multiply_reduce_fusion
  317.0 39.8 %psum.14 = f32[]{:T(128)} all-reduce(f32[]{:T(128)} %multiply_reduce_fusion), channel_id=1, replica_groups=mesh['dp'=4,'expert'=8] {'dp','expert'}, use_global_device_ids=true, to_apply=%region_4.5 | all-reduce | flops 1 | bytes 8 | tf_op jit(solution)/shard_map/psum | solution.py:103
  358.9 8.5 %multiply_subtract_fusion = (f32[8,352,256]{2,1,0:T(8,128)}, f32[8,352,256]{2,1,0:T(8,128)}, f32[8,352,256]{2,1,0:T(8,128)}) fusion(s16[8,354,256]{2,1,0:T(8,128)(2,1)} %all-to-all-done, f32[8,352]{1,0:T(8,128)S(1)} %exponential_multiply_fusion.6, f32[8,352]{1,0:T(8,128)S(1)} %exponential_multiply_fusion.4, s16[8,354,256]{2,1,0:T(8,128)(2,1)} %all-to-all-done.2, ...), kind=kLoop, calls=%fused_computation.44 | loop fusion | flops 17301504 | bytes 14462980 | tf_op jit(solution)/shard_map/sub | solution.py:21
  367.4 2.5 gather_fusion
  370.0 4.1 gather_fusion.1
  374.1 4.1 gather_fusion.2
  378.2 4.4 abs_reduce_fusion
  382.8 5.7 %clamp_convert_fusion = (s16[8,352,256]{2,1,0:T(8,128)(2,1)}, s16[8,352,256]{2,1,0:T(8,128)(2,1)}, s16[8,352,256]{2,1,0:T(8,128)(2,1)S(1)}) fusion(f32[8,352,256]{2,1,0:T(8,128)} %gather_fusion.2, f32[8,352]{1,0:T(8,128)S(1)} %get-tuple-element.14, pred[8]{0:T(512)(128)(4,1)S(1)} %compare_and_fusion, f32[8,352]{1,0:T(8,128)S(1)} %get-tuple-element.36, ...), kind=kLoop, calls=%fused_computation.36 | loop fusion | flops 10813440 | bytes 13009928 | tf_op jit(solution)/shard_map/convert_element_type | solution.py:40
  388.6 39.1 %all_to_all.35 = s16[8,354,256]{2,1,0:T(8,128)(2,1)S(1)} all-to-all(s16[8,354,256]{2,1,0:T(8,128)(2,1)S(1)} %pad_add_fusion.4), channel_id=1, replica_groups=mesh['dp'=4,'expert'=8] {'expert'}, dimensions={0} | all-to-all | bytes 2899968 | tf_op jit(solution)/shard_map/all_to_all | solution.py:63
  428.3 1.3 copy.44
  429.7 2.6 pad_add_fusion.6
  432.2 4.3 all-to-all-start.6
  436.6 2.7 pad_add_fusion.5
  439.3 32.9 %all-to-all-done.6 = s16[8,354,256]{2,1,0:T(8,128)(2,1)} async-done(((s16[8,354,256]{2,1,0:T(8,128)(2,1)}), s16[8,354,256]{2,1,0:T(8,128)(2,1)}, u32[]{:S(2)}, u32[]{:S(2)}) %all-to-all-start.6) | async-done | bytes 1450016 | tf_op jit(solution)/shard_map/all_to_all | solution.py:63
  472.3 4.6 all-to-all-start.5
  476.8 2.9 multiply_subtract_fusion.1
  480.6 1.9 multiply_bitcast_fusion
  482.4 3.2 copy.41
  485.7 4.2 broadcast_in_dim_reshape.11
  489.8 22.4 %all-to-all-done.5 = s16[8,354,256]{2,1,0:T(8,128)(2,1)} async-done(((s16[8,354,256]{2,1,0:T(8,128)(2,1)}), s16[8,354,256]{2,1,0:T(8,128)(2,1)}, u32[]{:S(2)}, u32[]{:S(2)}) %all-to-all-start.5) | async-done | bytes 1450016 | tf_op jit(solution)/shard_map/all_to_all | solution.py:63
  513.1 1.9 multiply_bitcast_fusion.1
  514.9 3.2 copy.40
  518.2 4.2 broadcast_in_dim_reshape.10
  522.4 3.2 copy.39
  525.6 4.2 broadcast_in_dim_reshape.9
  529.8 6.3 %copy.64 = bf16[1,1408,2048]{2,1,0:T(8,128)(2,1)} copy(bf16[1,1408,2048]{2,1,0:T(8,128)(2,1)} %bitcast.107) | data formatting | bytes 11534336
  (71 shorter events, 15.8 us)
Async XLA Ops:
  8.0 1.9 copy-start
  8.0 141.7 %reduce-scatter.4.cloned.1.call-start = ((), (), s32[]{:S(2)}) async-start(), calls=%async_computation.10 | async-start | bytes 14417920
  41.4 42.2 %all-to-all-start.3 = ((s16[8,354,256]{2,1,0:T(8,128)(2,1)}), s16[8,354,256]{2,1,0:T(8,128)(2,1)}, u32[]{:S(2)}, u32[]{:S(2)}) async-start(s16[8,354,256]{2,1,0:T(8,128)(2,1)} %pad_add_fusion.3), calls=%async_computation.3 | async-start | bytes 2949120 | tf_op jit(solution)/shard_map/all_to_all | solution.py:63
  83.5 40.0 %all-to-all-start.1 = ((s16[8,354,256]{2,1,0:T(8,128)(2,1)}), s16[8,354,256]{2,1,0:T(8,128)(2,1)}, u32[]{:S(2)}, u32[]{:S(2)}) async-start(s16[8,354,256]{2,1,0:T(8,128)(2,1)} %pad_add_fusion.1), calls=%async_computation.1 | async-start | bytes 2949120 | tf_op jit(solution)/shard_map/all_to_all | solution.py:63
  123.5 40.0 %all-to-all-start = ((s16[8,354,256]{2,1,0:T(8,128)(2,1)}), s16[8,354,256]{2,1,0:T(8,128)(2,1)}, u32[]{:S(2)}, u32[]{:S(2)}) async-start(s16[8,354,256]{2,1,0:T(8,128)(2,1)} %pad_add_fusion), calls=%async_computation | async-start | bytes 2949120 | tf_op jit(solution)/shard_map/all_to_all | solution.py:63
  159.0 8.8 %copy-start.2 = (bf16[64,128]{1,0:T(8,128)(2,1)S(1)}, bf16[64,128]{1,0:T(8,128)(2,1)}, u32[]{:S(2)}) copy-start(bf16[64,128]{1,0:T(8,128)(2,1)} %param.21) | copy-start | bytes 49156
  160.2 9.8 %copy-start.3 = (s32[8]{0:T(128)S(1)}, s32[8]{0:T(128)}, u32[]{:S(2)}) copy-start(s32[8]{0:T(128)} %param.25) | copy-start | bytes 100
  163.5 194.7 %all-to-all-start.2 = ((s16[8,354,256]{2,1,0:T(8,128)(2,1)}), s16[8,354,256]{2,1,0:T(8,128)(2,1)}, u32[]{:S(2)}, u32[]{:S(2)}) async-start(s16[8,354,256]{2,1,0:T(8,128)(2,1)} %pad_add_fusion.2), calls=%async_computation.2 | async-start | bytes 2949120 | tf_op jit(solution)/shard_map/all_to_all | solution.py:63
  167.8 143.6 %all-reduce.9.cloned.1.call-start = ((), (), s32[]{:S(2)}) async-start(), calls=%async_computation.8 | async-start | bytes 1048576 | tf_op jit(solution)/shard_map/psum | solution.py:102
  169.9 359.8 %all-gather.2.cloned.1.call-start = ((), (), s32[]{:S(2)}) async-start(), calls=%async_computation.9 | async-start | bytes 7208960 | tf_op jit(solution)/shard_map/all_gather | solution.py:67
  432.2 40.0 %all-to-all-start.6 = ((s16[8,354,256]{2,1,0:T(8,128)(2,1)}), s16[8,354,256]{2,1,0:T(8,128)(2,1)}, u32[]{:S(2)}, u32[]{:S(2)}) async-start(s16[8,354,256]{2,1,0:T(8,128)(2,1)} %pad_add_fusion.6), calls=%async_computation.6 | async-start | bytes 2949120 | tf_op jit(solution)/shard_map/all_to_all | solution.py:63
  472.3 40.0 %all-to-all-start.5 = ((s16[8,354,256]{2,1,0:T(8,128)(2,1)}), s16[8,354,256]{2,1,0:T(8,128)(2,1)}, u32[]{:S(2)}, u32[]{:S(2)}) async-start(s16[8,354,256]{2,1,0:T(8,128)(2,1)} %pad_add_fusion.5), calls=%async_computation.5 | async-start | bytes 2949120 | tf_op jit(solution)/shard_map/all_to_all | solution.py:63
  529.8 6.3 %copy-start.1 = (bf16[1,1152,1408]{2,1,0:T(8,128)(2,1)S(1)}, bf16[1,1152,1408]{2,1,0:T(8,128)(2,1)}, u32[]{:S(2)}) copy-start(bf16[1,1152,1408]{2,1,0:T(8,128)(2,1)} %param.14) | copy-start | bytes 9732100
Sparse Core Ops, SparseCore 0:
  35.0 114.7 reduce-scatter.3
  429.8 64.6 all-gather.1
Sparse Core Ops, SparseCore 1:
  174.1 137.3 all-reduce.8
where the time goes:
time: 546 us; the launch traced here: 544 us
  waiting for transfers between devices  281 us (51%)
  blocking collectives  78.9 us (14%)
  local copies, waits for them, and re-layouts  72.4 us (13%)
  other arithmetic  50.5 us (9%)
  starting transfers between devices  28.2 us (5%)
  between operations  18 us (3%)
  matrix products  14.9 us (3%)
    psum x1, waiting for transfers between devices, on_device(): router_grad = lax.psum(router_partial, ('dp', 'expert'))  141 us
    all_to_all x6, waiting for transfers between devices, exchange(): lax.all_to_all(payload, axis, split_axis=0, concat_axis=0, tiled=True)  117 us
    psum x1, blocking collectives, on_device(): expert_square = lax.psum(jnp.sum(gradient * gradient), ('dp', 'expert'))  39.8 us
    all_to_all x1, blocking collectives, exchange(): lax.all_to_all(payload, axis, split_axis=0, concat_axis=0, tiled=True)  39.1 us
    unnamed x28, local copies, waits for them, and re-layouts  35.7 us
    all_to_all x6, starting transfers between devices, exchange(): lax.all_to_all(payload, axis, split_axis=0, concat_axis=0, tiled=True)  28.1 us
    unnamed x4, waiting for transfers between devices  22 us
    dot_general x1, matrix products, on_device(): lax.dot_general(activations, masked_out, (((0,), (0,)), ((), ())), prefer...  12.9 us
  transfers between devices with their start and end apart: 9, of which 7 were waited for; matrix products, arithmetic and copies ran while one was open for 13% of the time, Pallas kernels for 0%

commit v1 on v0

--- a/solution.py
+++ b/solution.py
@@ -99,7 +99,7 @@
     )
     gradient = lax.psum_scatter(partial, "dp", scatter_dimension=0, tiled=True)
     moved_gradient = exchange(encode(to_pieces(gradient, groups)))
-    router_grad = lax.psum(router_partial, ("dp", "expert"))
+    router_grad = jnp.sum(lax.all_gather(router_partial, ("dp", "expert")), axis=0)
     expert_square = lax.psum(jnp.sum(gradient * gradient), ("dp", "expert"))
     total_square = expert_square + jnp.sum(router_grad * router_grad)
     clip_limit = 2.0 * math.sqrt(

time: 546 us -> 485 us (0.89)
  waiting for transfers between devices: 281 us -> 202 us
  blocking collectives: 78.9 us -> 91.1 us
  other arithmetic: 50.5 us -> 56.3 us
    psum x1 -> x0, waiting for transfers between devices: 141 us -> none  [on_device(): router_grad = lax.psum(router_partial, ('dp', 'expert'))]
    all_to_all x6, waiting for transfers between devices: 117 us -> 159 us  [exchange(): lax.all_to_all(payload, axis, split_axis=0, concat_axis=0, tiled=True)]
    unnamed x4, waiting for transfers between devices: 22 us -> 42.1 us
    psum x1, blocking collectives: 39.8 us -> 52 us  [on_device(): expert_square = lax.psum(jnp.sum(gradient * gradient), ('dp', 'expert'))]
    reduce_sum x0 -> x1, other arithmetic: none -> 6.9 us  [on_device(): jnp.sum(lax.all_gather(router_partial, ('dp', 'expert')), axis=0)]
    unnamed x28 -> x32, local copies, waits for them, and re-layouts: 35.7 us -> 36.9 us
  transfers between devices with their start and end apart: 9 -> 9, of which waited for: 7 -> 6; matrix products, arithmetic and copies ran while one was open for 13% -> 15% of each run, Pallas kernels for 0% -> 0%
where the time goes in v1:
time: 485 us; the launch traced here: 483 us
  waiting for transfers between devices  202 us (42%)
  blocking collectives  91.1 us (19%)
  local copies, waits for them, and re-layouts  73.7 us (15%)
  other arithmetic  56.3 us (12%)
  starting transfers between devices  28.3 us (6%)
  between operations  18 us (4%)
  matrix products  13.9 us (3%)
    all_to_all x6, waiting for transfers between devices, exchange(): lax.all_to_all(payload, axis, split_axis=0, concat_axis=0, tiled=True)  159 us
    psum x1, blocking collectives, on_device(): expert_square = lax.psum(jnp.sum(gradient * gradient), ('dp', 'expert'))  52 us
    unnamed x4, waiting for transfers between devices  42.1 us
    all_to_all x1, blocking collectives, exchange(): lax.all_to_all(payload, axis, split_axis=0, concat_axis=0, tiled=True)  39.1 us
    unnamed x32, local copies, waits for them, and re-layouts  36.9 us
    all_to_all x6, starting transfers between devices, exchange(): lax.all_to_all(payload, axis, split_axis=0, concat_axis=0, tiled=True)  28.2 us
    dot_general x1, matrix products, on_device(): lax.dot_general(activations, masked_out, (((0,), (0,)), ((), ())), prefer...  12.9 us
    sub x2, other arithmetic, adam_update(): weights_new = weights - learn_rate * (ratio + decay_weight * weights)  11.4 us
  transfers between devices with their start and end apart: 9, of which 6 were waited for; matrix products, arithmetic and copies ran while one was open for 15% of the time, Pallas kernels for 0%

profile of v1, /device:TPU:0, one launch (start us, length us, event | category | flops | bytes accessed | tf_op | source)
XLA Modules:
  0.0 482.8 jit_solution(5101101022983816664)
XLA Ops:
  9.9 12.9 %convolution_bitcast_fusion = f32[1408,2048]{0,1:T(8,128)} fusion(bf16[1,1152,2048]{2,1,0:T(8,128)(2,1)} %param.15, pred[1152]{0:T(1024)(128)(4,1)S(1)} %iota_compare_fusion, bf16[1,1152,1408]{2,1,0:T(8,128)(2,1)S(1)} %copy-done), kind=kOutput, calls=%fused_computation.3 | convolution fusion | flops 6646136832 | bytes 19498112 | tf_op jit(solution)/shard_map/dot_general | solution.py:97
  22.9 12.0 %copy.42 = f32[1408,2048]{1,0:T(8,128)} copy(f32[1408,2048]{0,1:T(8,128)} %convolution_bitcast_fusion) | data formatting | bytes 23068672
  37.0 3.1 copy.50
  42.3 1.2 pad_add_fusion.3
  43.5 6.4 %all-to-all-start.3 = ((s16[8,354,256]{2,1,0:T(8,128)(2,1)}), s16[8,354,256]{2,1,0:T(8,128)(2,1)}, u32[]{:S(2)}, u32[]{:S(2)}) async-start(s16[8,354,256]{2,1,0:T(8,128)(2,1)} %pad_add_fusion.3), calls=%async_computation.3 | async-start | bytes 2949120 | tf_op jit(solution)/shard_map/all_to_all | solution.py:63
  49.9 3.2 copy.47
  55.3 1.2 pad_add_fusion.1
  56.5 40.4 %all-to-all-done.3 = s16[8,354,256]{2,1,0:T(8,128)(2,1)} async-done(((s16[8,354,256]{2,1,0:T(8,128)(2,1)}), s16[8,354,256]{2,1,0:T(8,128)(2,1)}, u32[]{:S(2)}, u32[]{:S(2)}) %all-to-all-start.3) | async-done | bytes 1450016 | tf_op jit(solution)/shard_map/all_to_all | solution.py:63
  96.8 4.3 all-to-all-start.1
  101.1 3.2 copy.45
  106.5 1.2 pad_add_fusion
  107.8 44.3 %all-to-all-done.1 = s16[8,354,256]{2,1,0:T(8,128)(2,1)} async-done(((s16[8,354,256]{2,1,0:T(8,128)(2,1)}), s16[8,354,256]{2,1,0:T(8,128)(2,1)}, u32[]{:S(2)}, u32[]{:S(2)}) %all-to-all-start.1) | async-done | bytes 1450016 | tf_op jit(solution)/shard_map/all_to_all | solution.py:63
  152.1 4.4 all-to-all-start
  156.5 42.0 %reduce-scatter.4.cloned.1.call-done = f32[352,2048]{1,0:T(8,128)} async-done(((f32[1408,2048]{1,0:T(8,128)}), f32[352,2048]{1,0:T(8,128)}) %reduce-scatter.4.cloned.1.call-update) | async-done | bytes 2883600
  198.5 2.3 copy.43
  200.9 2.3 copy.36
  203.1 2.3 fusion.9
  205.5 2.3 fusion.12
  207.8 1.2 pad_add_fusion.2
  209.0 19.3 %all-to-all-done = s16[8,354,256]{2,1,0:T(8,128)(2,1)} async-done(((s16[8,354,256]{2,1,0:T(8,128)(2,1)}), s16[8,354,256]{2,1,0:T(8,128)(2,1)}, u32[]{:S(2)}, u32[]{:S(2)}) %all-to-all-start) | async-done | bytes 1450016 | tf_op jit(solution)/shard_map/all_to_all | solution.py:63
  228.3 4.3 all-to-all-start.2
  235.0 1.4 multiply_reduce_fusion
  236.5 52.0 %psum.7 = f32[]{:T(128)} all-reduce(f32[]{:T(128)} %multiply_reduce_fusion), channel_id=1, replica_groups=mesh['dp'=4,'expert'=8] {'dp','expert'}, use_global_device_ids=true, to_apply=%region_4.5 | all-reduce | flops 1 | bytes 8 | tf_op jit(solution)/shard_map/psum | solution.py:103
  289.3 6.9 %reduce_sum.28 = f32[64,2048]{1,0:T(8,128)S(1)} reduce(f32[32,64,2048]{2,1,0:T(8,128)} %bitcast.108, f32[]{:T(128)} %constant.81.clone.1), dimensions={0}, to_apply=%region_5.6 | reduce | flops 4063232 | bytes 17301508 | tf_op jit(solution)/shard_map/reduce_sum | solution.py:102
  298.3 8.5 %multiply_subtract_fusion = (f32[8,352,256]{2,1,0:T(8,128)}, f32[8,352,256]{2,1,0:T(8,128)}, f32[8,352,256]{2,1,0:T(8,128)}) fusion(s16[8,354,256]{2,1,0:T(8,128)(2,1)} %all-to-all-done, f32[8,352]{1,0:T(8,128)S(1)} %exponential_multiply_fusion.6, f32[8,352]{1,0:T(8,128)S(1)} %exponential_multiply_fusion.4, s16[8,354,256]{2,1,0:T(8,128)(2,1)} %all-to-all-done.2, ...), kind=kLoop, calls=%fused_computation.44 | loop fusion | flops 17301504 | bytes 14462980 | tf_op jit(solution)/shard_map/sub | solution.py:21
  306.8 2.5 gather_fusion
  309.3 4.1 gather_fusion.1
  313.4 4.1 gather_fusion.2
  317.6 4.4 abs_reduce_fusion
  322.1 5.7 %clamp_convert_fusion = (s16[8,352,256]{2,1,0:T(8,128)(2,1)}, s16[8,352,256]{2,1,0:T(8,128)(2,1)}, s16[8,352,256]{2,1,0:T(8,128)(2,1)S(1)}) fusion(f32[8,352,256]{2,1,0:T(8,128)} %gather_fusion.2, f32[8,352]{1,0:T(8,128)S(1)} %get-tuple-element.14, pred[8]{0:T(512)(128)(4,1)S(1)} %compare_and_fusion, f32[8,352]{1,0:T(8,128)S(1)} %get-tuple-element.36, ...), kind=kLoop, calls=%fused_computation.36 | loop fusion | flops 10813440 | bytes 13009928 | tf_op jit(solution)/shard_map/convert_element_type | solution.py:40
  327.9 39.1 %all_to_all.35 = s16[8,354,256]{2,1,0:T(8,128)(2,1)S(1)} all-to-all(s16[8,354,256]{2,1,0:T(8,128)(2,1)S(1)} %pad_add_fusion.4), channel_id=1, replica_groups=mesh['dp'=4,'expert'=8] {'expert'}, dimensions={0} | all-to-all | bytes 2899968 | tf_op jit(solution)/shard_map/all_to_all | solution.py:63
  367.6 1.4 copy.44
  369.0 2.6 pad_add_fusion.6
  371.6 4.3 all-to-all-start.6
  375.9 2.7 pad_add_fusion.5
  378.7 32.9 %all-to-all-done.6 = s16[8,354,256]{2,1,0:T(8,128)(2,1)} async-done(((s16[8,354,256]{2,1,0:T(8,128)(2,1)}), s16[8,354,256]{2,1,0:T(8,128)(2,1)}, u32[]{:S(2)}, u32[]{:S(2)}) %all-to-all-start.6) | async-done | bytes 1450016 | tf_op jit(solution)/shard_map/all_to_all | solution.py:63
  411.6 4.5 all-to-all-start.5
  416.2 2.9 multiply_subtract_fusion.1
  419.9 1.9 multiply_bitcast_fusion
  421.7 3.2 copy.41
  425.0 4.2 broadcast_in_dim_reshape.11
  429.2 22.4 %all-to-all-done.5 = s16[8,354,256]{2,1,0:T(8,128)(2,1)} async-done(((s16[8,354,256]{2,1,0:T(8,128)(2,1)}), s16[8,354,256]{2,1,0:T(8,128)(2,1)}, u32[]{:S(2)}, u32[]{:S(2)}) %all-to-all-start.5) | async-done | bytes 1450016 | tf_op jit(solution)/shard_map/all_to_all | solution.py:63
  452.4 1.9 multiply_bitcast_fusion.1
  454.3 3.2 copy.40
  457.5 4.2 broadcast_in_dim_reshape.10
  461.7 3.2 copy.39
  464.9 4.2 broadcast_in_dim_reshape.9
  469.1 6.3 %copy.63 = bf16[1,1408,2048]{2,1,0:T(8,128)(2,1)} copy(bf16[1,1408,2048]{2,1,0:T(8,128)(2,1)} %bitcast.109) | data formatting | bytes 11534336
  (76 shorter events, 16.1 us)
Async XLA Ops:
  8.0 1.9 copy-start
  8.0 190.5 %reduce-scatter.4.cloned.1.call-start = ((), (), s32[]{:S(2)}) async-start(), calls=%async_computation.10 | async-start | bytes 14417920
  34.9 1.0 copy-start.3
  34.9 1.0 copy-start.4
  34.9 254.3 %all-gather.6.cloned.1.call-start = ((), (), s32[]{:S(2)}) async-start(), calls=%async_computation.9 | async-start | bytes 17301504 | tf_op jit(solution)/shard_map/all_gather | solution.py:102
  43.5 53.3 %all-to-all-start.3 = ((s16[8,354,256]{2,1,0:T(8,128)(2,1)}), s16[8,354,256]{2,1,0:T(8,128)(2,1)}, u32[]{:S(2)}, u32[]{:S(2)}) async-start(s16[8,354,256]{2,1,0:T(8,128)(2,1)} %pad_add_fusion.3), calls=%async_computation.3 | async-start | bytes 2949120 | tf_op jit(solution)/shard_map/all_to_all | solution.py:63
  96.8 55.3 %all-to-all-start.1 = ((s16[8,354,256]{2,1,0:T(8,128)(2,1)}), s16[8,354,256]{2,1,0:T(8,128)(2,1)}, u32[]{:S(2)}, u32[]{:S(2)}) async-start(s16[8,354,256]{2,1,0:T(8,128)(2,1)} %pad_add_fusion.1), calls=%async_computation.1 | async-start | bytes 2949120 | tf_op jit(solution)/shard_map/all_to_all | solution.py:63
  152.1 76.2 %all-to-all-start = ((s16[8,354,256]{2,1,0:T(8,128)(2,1)}), s16[8,354,256]{2,1,0:T(8,128)(2,1)}, u32[]{:S(2)}, u32[]{:S(2)}) async-start(s16[8,354,256]{2,1,0:T(8,128)(2,1)} %pad_add_fusion), calls=%async_computation | async-start | bytes 2949120 | tf_op jit(solution)/shard_map/all_to_all | solution.py:63
  207.8 24.9 %copy-start.5 = (s32[8]{0:T(128)S(1)}, s32[8]{0:T(128)}, u32[]{:S(2)}) copy-start(s32[8]{0:T(128)} %param.25) | copy-start | bytes 100
  228.3 60.1 %all-to-all-start.2 = ((s16[8,354,256]{2,1,0:T(8,128)(2,1)}), s16[8,354,256]{2,1,0:T(8,128)(2,1)}, u32[]{:S(2)}, u32[]{:S(2)}) async-start(s16[8,354,256]{2,1,0:T(8,128)(2,1)} %pad_add_fusion.2), calls=%async_computation.2 | async-start | bytes 2949120 | tf_op jit(solution)/shard_map/all_to_all | solution.py:63
  232.6 236.5 %all-gather.4.cloned.1.call-start = ((), (), s32[]{:S(2)}) async-start(), calls=%async_computation.8 | async-start | bytes 7208960 | tf_op jit(solution)/shard_map/all_gather | solution.py:67
  296.2 10.6 %copy-start.2 = (f32[64,2048]{1,0:T(8,128)}, f32[64,2048]{1,0:T(8,128)S(1)}, u32[]{:S(2)}) copy-start(f32[64,2048]{1,0:T(8,128)S(1)} %reduce_sum.28) | copy-start | bytes 1572868
  371.6 40.0 %all-to-all-start.6 = ((s16[8,354,256]{2,1,0:T(8,128)(2,1)}), s16[8,354,256]{2,1,0:T(8,128)(2,1)}, u32[]{:S(2)}, u32[]{:S(2)}) async-start(s16[8,354,256]{2,1,0:T(8,128)(2,1)} %pad_add_fusion.6), calls=%async_computation.6 | async-start | bytes 2949120 | tf_op jit(solution)/shard_map/all_to_all | solution.py:63
  411.6 40.0 %all-to-all-start.5 = ((s16[8,354,256]{2,1,0:T(8,128)(2,1)}), s16[8,354,256]{2,1,0:T(8,128)(2,1)}, u32[]{:S(2)}, u32[]{:S(2)}) async-start(s16[8,354,256]{2,1,0:T(8,128)(2,1)} %pad_add_fusion.5), calls=%async_computation.5 | async-start | bytes 2949120 | tf_op jit(solution)/shard_map/all_to_all | solution.py:63
  469.1 6.3 %copy-start.1 = (bf16[1,1152,1408]{2,1,0:T(8,128)(2,1)S(1)}, bf16[1,1152,1408]{2,1,0:T(8,128)(2,1)}, u32[]{:S(2)}) copy-start(bf16[1,1152,1408]{2,1,0:T(8,128)(2,1)} %param.14) | copy-start | bytes 9732100
Sparse Core Ops, SparseCore 0:
  35.1 163.4 reduce-scatter.3
  369.1 64.6 all-gather.3
Sparse Core Ops, SparseCore 1:
  39.0 195.6 all-gather.5
